TPU v7x, 32 devices: a whole 2x2x4 slice. The times are simulated.
32 devices in a mesh: section: 4 (over z), tensor: 8 (over y, x, core).
Axes of the slice: x: 2, y: 2, z: 4, core: 2. Of those that a mesh axis runs over, the one named last changes fastest.
Arguments:
- hidden_state: bfloat16 [64, 8192], P('section'), may hold values from -6 to 6
- norm_gain: float32 [8192], replicated, may hold values from 0.5 to 1.5
- wq_old: bfloat16 [8192, 8192], P('section', 'tensor'), may hold values from -0.0625 to 0.0625
- wkv_old: bfloat16 [8192, 2048], P('tensor', 'section'), may hold values from -0.0625 to 0.0625
- kv_old: bfloat16 [8, 4096, 16, 256], P('section', 'tensor'), may hold values from -241 to 241
- page_table: int32 [64, 64], replicated, may hold values from 0 to 4095, as said below
- lengths: int32 [64], replicated, may hold values from 1 to 1023
Outputs:
- context: bfloat16 [64, 8192], P('section', 'tensor')
- kv_new: bfloat16 [64, 8, 1024, 256], P('section', 'tensor')
- wq_new: bfloat16 [8192, 8192], P(None, 'tensor')
- wkv_new: bfloat16 [8192, 2048], P(None, 'tensor')
Inputs may be any that keep to these rules, and one draw needn't show every extreme that they name: `page_table`: every pool page belongs to exactly one page of one request. Each block of 512 consecutive pool pages holds exactly 8 pages of every request.
All inputs are finite; a program needn't handle non-finite values.
Results may differ from a plain program's by a relative error of at most 0.0075.
The roundings to bfloat16 on the way count: a program that leaves them out, or rounds other values in their place, can miss the bound.
Values may be sent and summed in bfloat16 or wider, within the bound.
A program may use at most 128 MiB of HBM per device.

v0:
```python
import jax
import jax.numpy as jnp
from jax import lax
from jax.sharding import PartitionSpec as P

KV_HEADS = 8
HEAD_DIM = 128


EPSILON = 1e-05
ROPE_BASE = 500000.0


def broadcast(block, axis, source):
    block = jnp.where(lax.axis_index(axis) == source, block, jnp.zeros_like(block))
    return lax.psum(block, axis)


def rotate(values, position, head_dim):
    half = head_dim // 2
    frequency = ROPE_BASE ** (-(jnp.arange(half, dtype=jnp.float32) * 2.0 / head_dim))
    angles = position.astype(jnp.float32)[:, None] * frequency[None, :]
    cosine = jnp.cos(angles)[:, None, :]
    sine = jnp.sin(angles)[:, None, :]
    first = values[..., :half]
    second = values[..., half:]
    return jnp.concatenate(
        [first * cosine - second * sine, second * cosine + first * sine], axis=-1
    )


def shards(hidden_state, norm_gain, wq_old, wkv_old, kv_old, page_table, lengths):
    sections = lax.axis_size("section")
    tensors = lax.axis_size("tensor")
    section_id = lax.axis_index("section")
    tensor_id = lax.axis_index("tensor")
    rows = hidden_state.shape[0]
    head_dim = HEAD_DIM
    width = 2 * head_dim
    local_heads = KV_HEADS // sections
    repeats = tensors // KV_HEADS
    queries_here = wq_old.shape[1] // head_dim
    pool_dev = kv_old.shape[1]
    page = kv_old.shape[2]
    total_reqs = page_table.shape[0]
    per_block = page_table.shape[1] // tensors
    slots = page_table.shape[1] * page
    widened = hidden_state.astype(jnp.float32)
    scale = lax.rsqrt(jnp.mean(widened * widened, axis=1, keepdims=True) + EPSILON)
    normed = (widened * scale * norm_gain[None, :]).astype(jnp.bfloat16)
    wq_new = lax.all_gather(wq_old, "section", axis=0, tiled=True)
    spread = lax.all_to_all(normed, "section", split_axis=1, concat_axis=0, tiled=True)
    query = lax.psum_scatter(
        jnp.dot(spread, wq_old, preferred_element_type=jnp.float32),
        "section",
        scatter_dimension=0,
        tiled=True,
    )
    kv_rows = lax.all_gather(wkv_old, "tensor", axis=0, tiled=True)
    head_needed = tensor_id * KV_HEADS // tensors
    offset = jnp.clip(head_needed - section_id * local_heads, 0, local_heads - 1)
    own_part = lax.dynamic_slice_in_dim(kv_rows, offset * width, width, 1)
    wkv_new = broadcast(own_part, "section", head_needed // local_heads)
    owner = page_table // pool_dev
    blocks = jnp.arange(tensors, dtype=jnp.int32)
    onehot = (owner[:, :, None] == blocks[None, None, :]).astype(jnp.int32)
    ranks = jnp.sum((jnp.cumsum(onehot, axis=1) - 1) * onehot, axis=2)
    mine = owner == tensor_id
    wanted = ranks[:, :, None] == jnp.arange(per_block, dtype=jnp.int32)[None, None, :]
    picks = (mine[:, :, None] & wanted).astype(jnp.int32)
    spots = jnp.sum(picks * (page_table % pool_dev)[:, :, None], axis=1)
    pages = jnp.take(kv_old, spots.reshape(-1), axis=1)
    pages = pages.reshape(local_heads, total_reqs, per_block * page, width)
    copied = jnp.repeat(pages, repeats, axis=0)
    arrived = lax.all_to_all(
        lax.all_to_all(copied, "section", split_axis=1, concat_axis=0, tiled=True),
        "tensor",
        split_axis=0,
        concat_axis=2,
        tiled=True,
    )
    arrived = arrived.reshape(rows, tensors * per_block, page, width)
    source = lax.dynamic_slice_in_dim(owner * per_block + ranks, section_id * rows, rows, 0)
    ordered = jnp.take_along_axis(arrived, source[:, :, None, None], axis=1).reshape(
        rows, slots, width
    )
    my_lengths = lax.dynamic_slice_in_dim(lengths, section_id * rows, rows, 0)
    fresh = jnp.dot(normed, wkv_new, preferred_element_type=jnp.float32)
    fresh_key = rotate(fresh[:, None, :head_dim], my_lengths, head_dim)[:, 0]
    fresh = jnp.concatenate([fresh_key, fresh[:, head_dim:]], axis=1).astype(jnp.bfloat16)
    slot_ids = jnp.arange(slots, dtype=jnp.int32)
    written = (slot_ids[None, :] == my_lengths[:, None])[:, :, None]
    cache = jnp.where(written, fresh[:, None, :], ordered)
    query = rotate(query.reshape(rows, queries_here, head_dim), my_lengths, head_dim).astype(
        jnp.bfloat16
    )
    scores = jnp.einsum(
        "rgd,rsd->rgs", query, cache[:, :, :head_dim], preferred_element_type=jnp.float32
    ) * head_dim ** (-0.5)
    seen = (slot_ids[None, :] <= my_lengths[:, None])[:, None, :]
    peak = jnp.max(jnp.where(seen, scores, -jnp.inf), axis=2, keepdims=True)
    weights = jnp.where(seen, jnp.exp(scores - peak), 0.0)
    probs = (weights / jnp.sum(weights, axis=2, keepdims=True)).astype(jnp.bfloat16)
    mixed = jnp.einsum(
        "rgs,rsd->rgd", probs, cache[:, :, head_dim:], preferred_element_type=jnp.float32
    )
    context = mixed.astype(jnp.bfloat16).reshape(rows, queries_here * head_dim)
    return (context, cache[:, None], wq_new, wkv_new)


def solution(mesh):
    placed = (
        P("section", None),
        P(),
        P("section", "tensor"),
        P("tensor", "section"),
        P("section", "tensor", None, None),
        P(),
        P(),
    )
    return jax.shard_map(
        shards,
        mesh=mesh,
        in_specs=placed,
        out_specs=(
            P("section", "tensor"),
            P("section", "tensor", None, None),
            P(None, "tensor"),
            P(None, "tensor"),
        ),
        check_vma=False,
    )
```

profile of v0, /device:TPU:0, one launch (start us, length us, event | category | flops | bytes accessed | tf_op | source)
XLA Modules:
  0.0 690.0 jit_solution(9300361213904541417)
XLA Ops:
  8.0 0.0 all-gather.3.cloned.1.call-start
  8.0 0.7 all-gather.3.cloned.1.call-update
  8.7 1.1 fusion.20
  9.9 1.1 fusion.22
  11.0 0.7 copy.68
  11.7 6.3 all-to-all-start
  18.0 0.0 reduce-scatter.2.cloned.1.call-start
  18.0 8.9 %all-to-all-done = bf16[16,4,2048]{2,0,1:T(8,128)(2,1)S(1)} async-done(((bf16[16,4,2048]{2,0,1:T(8,128)(2,1)}), bf16[16,4,2048]{2,0,1:T(8,128)(2,1)S(1)}, u32[]{:S(2)}, u32[]{:S(2)}) %all-to-all-start) | async-done | bytes 262176 | tf_op jit(solution)/shard_map/all_to_all | solution.py:52
  26.9 3.8 fusion.45
  30.7 0.0 reduce-scatter.2.cloned.1.call-update
  30.7 0.0 copy-start.1
  30.7 0.0 all-reduce.2.cloned.1.call-start
  30.8 36.9 %all-gather.3.cloned.1.call-done = bf16[8192,512]{1,0:T(8,128)(2,1)} async-done(((bf16[1024,512]{1,0:T(8,128)(2,1)}), bf16[8192,512]{1,0:T(8,128)(2,1)}) %all-gather.3.cloned.1.call-update) | async-done | bytes 8388624 | tf_op jit(solution)/shard_map/all_gather | solution.py:59
  67.7 4.9 dynamic-slice_select_fusion
  72.6 0.0 all-reduce.2.cloned.1.call-update
  72.7 0.0 all-gather.5.cloned.1.call-start
  72.7 0.5 all-gather.5.cloned.1.call-update
  73.3 0.0 copy-done.1
  73.3 0.1 copy.48
  73.4 2.3 select_reduce_fusion.1
  75.7 2.2 select_reduce_fusion
  77.9 0.1 reshape.269
  78.0 23.4 %gather_fusion = bf16[512,2,16,256]{3,2,1,0:T(8,128)(2,1)} fusion(bf16[2,512,16,256]{3,2,1,0:T(8,128)(2,1)} %param.11, s32[1024]{0:T(1024)S(1)} %pad_clamp_fusion), kind=kCustom, calls=%fused_computation | custom fusion | bytes 16779264 | tf_op jit(solution)/shard_map/jit(_take)/gather | solution.py:72
  101.4 7.4 %copy.55 = bf16[2,512,16,256]{3,2,1,0:T(8,128)(2,1)} copy(bf16[2,512,16,256]{3,2,0,1:T(8,128)(2,1)} %bitcast.56) | data formatting | bytes 16777216 | tf_op jit(solution)/shard_map/jit(_take)/gather | solution.py:72
  108.9 0.1 copy.53
  109.0 0.1 copy.54
  109.1 7.5 %bitcast_select_fusion.1 = bf16[2,64,128,256]{3,2,1,0:T(8,128)(2,1)} fusion(pred[64,128]{1,0:T(8,128)(4,1)S(1)} %copy.54, bf16[2,64,128,256]{3,2,1,0:T(8,128)(2,1)} %bitcast.54), kind=kLoop, calls=%fused_computation.5 | loop fusion | flops 4194304 | bytes 16785408 | tf_op jit(solution)/shard_map/jit(_take)/select_n | solution.py:72
  116.6 8.0 %copy.56 = bf16[2,64,128,256]{3,2,0,1:T(8,128)(2,1)} copy(bf16[2,64,128,256]{3,2,1,0:T(8,128)(2,1)} %bitcast_select_fusion.1) | data formatting | bytes 16777216 | tf_op jit(solution)/shard_map/jit(_take)/select_n | solution.py:72
  124.6 369.9 %all_to_all.52 = bf16[2,64,128,256]{3,2,0,1:T(8,128)(2,1)} all-to-all(bf16[2,64,128,256]{3,2,0,1:T(8,128)(2,1)} %copy.56), channel_id=1, replica_groups=mesh['section'=4,'tensor'=8] {'section'}, dimensions={1} | all-to-all | bytes 16777216 | tf_op jit(solution)/shard_map/all_to_all | solution.py:76
  494.4 7.9 %copy.58 = bf16[4,2,16,128,256]{4,3,2,1,0:T(8,128)(2,1)} copy(bf16[4,2,16,128,256]{4,3,1,2,0:T(8,128)(2,1)} %bitcast.57) | data formatting | bytes 16777216 | tf_op jit(solution)/shard_map/all_to_all | solution.py:76
  502.3 5.3 all-to-all-start.2
  507.6 0.1 bitcast_or_fusion
  507.7 0.1 copy.60
  507.7 0.1 reshape.281
  507.8 0.1 compare_and_fusion.1
  507.9 0.1 copy.52
  508.0 0.2 broadcast_in_dim.106
  508.2 0.3 broadcast_in_dim.107
  508.6 0.0 copy-done.2
  508.6 0.1 fusion.43
  508.7 0.1 multiply_cosine_fusion.1
  508.8 0.1 iota_compare_fusion.4
  508.9 0.0 reduce-scatter.2.cloned.1.call-done
  508.9 0.9 copy.64
  509.8 0.1 subtract_convert_fusion
  509.9 0.0 all-reduce.2.cloned.1.call-done
  509.9 2.8 fusion.46
  512.7 0.1 fusion.40
  512.9 0.1 pad_maximum_fusion
  513.0 88.5 %all-to-all-done.2 = bf16[8,16,128,256]{3,2,1,0:T(8,128)(2,1)} async-done(((bf16[8,16,128,256]{3,2,1,0:T(8,128)(2,1)}), bf16[8,16,128,256]{3,2,1,0:T(8,128)(2,1)}, u32[]{:S(2)}, u32[]{:S(2)}) %all-to-all-start.2) | async-done | bytes 8388640 | tf_op jit(solution)/shard_map/all_to_all | solution.py:75
  601.4 7.9 %copy.59 = bf16[1,16,8,128,256]{4,3,2,1,0:T(8,128)(2,1)} copy(bf16[1,16,8,128,256]{4,3,1,2,0:T(8,128)(2,1)} %bitcast.14) | data formatting | bytes 16777216 | tf_op jit(solution)/shard_map/all_to_all | solution.py:75
  609.3 14.7 %gather_fusion.1 = bf16[1024,16,256]{2,1,0:T(8,128)(2,1)} fusion(bf16[16,64,16,256]{3,2,1,0:T(8,128)(2,1)} %bitcast.55, s32[1024]{0:T(1024)S(1)} %reshape.281), kind=kCustom, calls=%fused_computation.1 | custom fusion | bytes 16785408 | tf_op jit(solution)/shard_map/jit(take_along_axis)/gather | solution.py:84
  624.0 7.8 %fusion.1 = bf16[16,1024,256]{2,1,0:T(8,128)(2,1)S(1)} fusion(pred[16,1024]{1,0:T(8,128)(4,1)S(1)} %broadcast_in_dim.107, pred[16,1024]{1,0:T(8,128)(4,1)S(1)} %get-tuple-element.15, bf16[16,256]{1,0:T(8,128)(2,1)S(1)} %pad_maximum_fusion, bf16[16,1024,256]{2,1,0:T(8,128)(2,1)} %bitcast.49), kind=kLoop, calls=%fused_computation.4 | loop fusion | flops 8388608 | bytes 16818176 | tf_op jit(solution)/shard_map/jit(_where)/select_n | solution.py:93
  631.8 1.2 fusion.9
  633.0 2.9 fusion.44
  635.9 0.7 fusion.15
  636.6 0.6 copy.69
  637.3 0.0 slice-done
  637.3 0.0 slice-done.1
  637.3 6.6 select_select_fusion
  643.9 22.3 %all-gather.5.cloned.1.call-done = bf16[8192,1024]{1,0:T(8,128)(2,1)} async-done(((bf16[2048,1024]{1,0:T(8,128)(2,1)}), bf16[8192,1024]{1,0:T(8,128)(2,1)}) %all-gather.5.cloned.1.call-update) | async-done | bytes 16777232 | tf_op jit(solution)/shard_map/all_gather | solution.py:51
  666.2 14.2 %copy.72 = bf16[8192,1024]{1,0:T(8,128)(2,1)} copy(bf16[8192,1024]{1,0:T(8,128)(2,1)} %all-gather.5.cloned.1.call-done) | data formatting | bytes 33554432
  680.4 0.0 copy-done
  680.4 2.0 copy.73
  (15 shorter events, 0.1 us)
Async XLA Ops:
  8.0 59.7 %all-gather.3.cloned.1.call-start = ((), (), s32[]{:S(2)}) async-start(), calls=%async_computation.5 | async-start | bytes 9437184 | tf_op jit(solution)/shard_map/all_gather | solution.py:59
  11.7 15.3 %all-to-all-start = ((bf16[16,4,2048]{2,0,1:T(8,128)(2,1)}), bf16[16,4,2048]{2,0,1:T(8,128)(2,1)S(1)}, u32[]{:S(2)}, u32[]{:S(2)}) async-start(bf16[16,4,2048]{2,0,1:T(8,128)(2,1)} %bitcast.45), calls=%async_computation | async-start | bytes 524288 | tf_op jit(solution)/shard_map/all_to_all | solution.py:52
  18.0 490.9 %reduce-scatter.2.cloned.1.call-start = ((), (), s32[]{:S(2)}) async-start(), calls=%async_computation.4 | async-start | bytes 327680 | tf_op jit(solution)/shard_map/reduce_scatter | solution.py:53
  30.7 42.5 %copy-start.1 = (s32[64,64]{1,0:T(8,128)S(1)}, s32[64,64]{1,0:T(8,128)}, u32[]{:S(2)}) copy-start(s32[64,64]{1,0:T(8,128)} %param.12) | copy-start | bytes 49156
  30.7 479.2 %all-reduce.2.cloned.1.call-start = ((), (), s32[]{:S(2)}) async-start(), calls=%async_computation.6 | async-start | bytes 8388608 | tf_op jit(solution)/shard_map/psum | solution.py:16
  72.7 593.5 %all-gather.5.cloned.1.call-start = ((), (), s32[]{:S(2)}) async-start(), calls=%async_computation.7 | async-start | bytes 20971520 | tf_op jit(solution)/shard_map/all_gather | solution.py:51
  502.3 6.3 copy-start.2
  502.3 99.1 %all-to-all-start.2 = ((bf16[8,16,128,256]{3,2,1,0:T(8,128)(2,1)}), bf16[8,16,128,256]{3,2,1,0:T(8,128)(2,1)}, u32[]{:S(2)}, u32[]{:S(2)}) async-start(bf16[8,16,128,256]{3,2,1,0:T(8,128)(2,1)} %bitcast.53), calls=%async_computation.3 | async-start | bytes 16777216 | tf_op jit(solution)/shard_map/all_to_all | solution.py:75
  624.0 13.3 %slice-start = ((s8[8388608]{0:T(1024)(128)(4,1)}), s8[4194304]{0:T(1024)(128)(4,1)S(1)}, s32[]{:S(2)}) async-start(s8[8388608]{0:T(1024)(128)(4,1)} %bitcast.50), calls=%async_computation.8 | async-start | bytes 8388608
  624.0 13.3 %slice-start.1 = ((s8[8388608]{0:T(1024)(128)(4,1)}), s8[4194304]{0:T(1024)(128)(4,1)S(1)}, s32[]{:S(2)}) async-start(s8[8388608]{0:T(1024)(128)(4,1)} %bitcast.50), calls=%async_computation.9 | async-start | bytes 8388608
  666.2 14.2 %copy-start = (bf16[8192,256]{1,0:T(8,128)(2,1)S(1)}, bf16[8192,256]{1,0:T(8,128)(2,1)}, u32[]{:S(2)}) copy-start(bf16[8192,256]{1,0:T(8,128)(2,1)} %all-reduce.2.cloned.1.call-done) | copy-start | bytes 12582916
Sparse Core Ops, SparseCore 0:
  10.7 56.9 all-gather.2
Sparse Core Ops, SparseCore 1:
  30.8 19.0 reduce-scatter.1
  72.8 276.7 all-reduce.1
  350.9 315.2 all-gather.4
where the time goes:
time: 691 us; the launch traced here: 690 us
  blocking collectives  370 us (54%)
  waiting for transfers between devices  158 us (23%)
  local copies, waits for them, and re-layouts  88.8 us (13%)
  other arithmetic  37.3 us (5%)
  between operations  15.8 us (2%)
  starting transfers between devices  11.7 us (2%)
  matrix products  8.55 us (1%)
    all_to_all x1, blocking collectives, shards(): lax.all_to_all(copied, 'section', split_axis=1, concat_axis=0, tiled=True)  370 us
    all_to_all x1, waiting for transfers between devices, shards(): lax.all_to_all(lax.all_to_all(copied, 'section', split_axis=1, concat_axi...  88.5 us
    all_gather x1, waiting for transfers between devices, shards(): kv_rows = lax.all_gather(wkv_old, 'tensor', axis=0, tiled=True)  36.9 us
    gather x2, local copies, waits for them, and re-layouts, shards(): pages = jnp.take(kv_old, spots.reshape(-1), axis=1)  30.9 us
    all_gather x1, waiting for transfers between devices, shards(): wq_new = lax.all_gather(wq_old, 'section', axis=0, tiled=True)  22.3 us
    unnamed x15, local copies, waits for them, and re-layouts  17.8 us
    gather x3, local copies, waits for them, and re-layouts, shards(): jnp.take_along_axis(arrived, source[:, :, None, None], axis=1)  14.8 us
    select_n x2, other arithmetic, shards(): cache = jnp.where(written, fresh[:, None, :], ordered)  14.4 us
  transfers between devices with their start and end apart: 6, of which 4 were waited for; matrix products, arithmetic and copies ran while one was open for 17% of the time, Pallas kernels for 0%

commit v1 on v0

v1 whole, which is shorter than its diff:
```python
import functools

import jax
import jax.numpy as jnp
from jax import lax
from jax.experimental import pallas as pl
from jax.experimental.pallas import tpu as pltpu
from jax.sharding import PartitionSpec as P

KV_HEADS = 8
HEAD_DIM = 128


EPSILON = 1e-05
ROPE_BASE = 500000.0
MESH = pl.DeviceIdType.MESH
CHUNKS = 8


def rotate(values, position, head_dim):
    half = head_dim // 2
    frequency = ROPE_BASE ** (-(jnp.arange(half, dtype=jnp.float32) * 2.0 / head_dim))
    angles = position.astype(jnp.float32)[:, None] * frequency[None, :]
    cosine = jnp.cos(angles)[:, None, :]
    sine = jnp.sin(angles)[:, None, :]
    first = values[..., :half]
    second = values[..., half:]
    return jnp.concatenate(
        [first * cosine - second * sine, second * cosine + first * sine], axis=-1
    )


def pick_kernel(count, spots_ref, kv_ref, out_ref):
    base = pl.program_id(1) * count

    def step(i, carry):
        out_ref[0, 0, i] = kv_ref[0, spots_ref[base + i]]
        return carry

    lax.fori_loop(0, count, step, 0, unroll=8)


def pick_pages(kv_old, spots, sections):
    heads, pool, page, width = kv_old.shape
    count = spots.shape[0] // sections
    return pl.pallas_call(
        functools.partial(pick_kernel, count),
        out_shape=jax.ShapeDtypeStruct((sections, heads, count, page, width), kv_old.dtype),
        grid_spec=pltpu.PrefetchScalarGridSpec(
            num_scalar_prefetch=1,
            grid=(heads, sections),
            in_specs=[pl.BlockSpec((1, pool, page, width), lambda h, s, spots: (h, 0, 0, 0))],
            out_specs=pl.BlockSpec(
                (1, 1, count, page, width), lambda h, s, spots: (s, h, 0, 0, 0)
            ),
        ),
        compiler_params=pltpu.CompilerParams(vmem_limit_bytes=40 * 2**20),
        name="pick_pages",
    )(spots, kv_old)


def exchange_kernel(
    sections,
    tensors,
    local_heads,
    repeats,
    normed_ref,
    wq_ref,
    pages_ref,
    wkv_ref,
    query_ref,
    arrived_ref,
    wkv_new_ref,
    wq_new_ref,
    stage_ref,
    stage_wkv_ref,
    spread,
    part,
    partial_in,
    spread_send,
    spread_recv,
    part_send,
    part_recv,
    page_send,
    page_recv,
    wkv_send,
    wkv_recv,
    local_sem,
    own_send,
    relay_send,
    wq_recv,
    stage_send,
    stage_recv,
):
    me = lax.axis_index("section")
    mine = lax.axis_index("tensor")
    depth, columns = wq_ref.shape
    width = wkv_new_ref.shape[1]
    block = wkv_ref.shape[0]

    def spread_copy(other, slot):
        return pltpu.make_async_remote_copy(
            normed_ref.at[:, pl.ds(pl.multiple_of(other * depth, 128), depth)],
            spread.at[me],
            spread_send.at[slot],
            spread_recv.at[me],
            device_id=(other, mine),
            device_id_type=MESH,
        )

    def part_copy(other, slot):
        return pltpu.make_async_remote_copy(
            part.at[other],
            partial_in.at[me],
            part_send.at[slot],
            part_recv.at[me],
            device_id=(other, mine),
            device_id_type=MESH,
        )

    chunks = own_send.shape[1]
    chunk = depth // chunks

    def wq_rows(owner, i):
        return wq_new_ref.at[pl.ds(pl.multiple_of(owner * depth + i * chunk, 16), chunk), :]

    def own_copy(side, i):
        return pltpu.make_async_remote_copy(
            wq_ref.at[pl.ds(pl.multiple_of(i * chunk, 16), chunk), :],
            wq_rows(me, i),
            own_send.at[side, i],
            wq_recv.at[me, i],
            device_id=(me + (1, -1)[side], mine),
            device_id_type=MESH,
        )

    def relay_copy(owner, side, i):
        return pltpu.make_async_remote_copy(
            wq_rows(owner, i),
            wq_rows(owner, i),
            relay_send.at[owner, i],
            wq_recv.at[owner, i],
            device_id=(me + (1, -1)[side], mine),
            device_id_type=MESH,
        )

    onward = (me + 1 < sections, me > 0)

    def each_chunk(act):
        def run(i, carry):
            act(i)
            return carry

        lax.fori_loop(0, chunks, run, 0)

    for step in range(1, sections):
        spread_copy(lax.rem(me + step, sections), step).start()

    def send_own(i):
        for side in range(2):
            pl.when(onward[side])(lambda: own_copy(side, i).start())

    def stage_copy(origin, other, step, which):
        pairs = (
            (pages_ref.at[other], stage_ref.at[origin]),
            (wkv_ref, stage_wkv_ref.at[origin]),
        )
        return pltpu.make_async_remote_copy(
            *pairs[which],
            stage_send.at[which, step],
            stage_recv.at[which, origin],
            device_id=(other, mine),
            device_id_type=MESH,
        )

    for step in range(1, sections):
        for which in range(2):
            stage_copy(me, lax.rem(me + step, sections), step, which).start()
    each_chunk(send_own)
    keep = pltpu.make_async_copy(
        wq_ref, wq_new_ref.at[pl.ds(pl.multiple_of(me * depth, 16), depth), :], local_sem.at[2]
    )
    keep.start()
    spread[me] = normed_ref[:, pl.ds(pl.multiple_of(me * depth, 128), depth)]

    def page_copy(step, head, copy):
        slot = (step * local_heads + head) * repeats + copy
        other = lax.rem(me + step, sections)
        target = (other * local_heads + head) * repeats + copy
        source = pages_ref.at[me, head] if step == 0 else stage_ref.at[other, head]
        here = (source, arrived_ref.at[mine])
        remote = pltpu.make_async_remote_copy(
            *here,
            page_send.at[slot],
            page_recv.at[mine],
            device_id=(me, target),
            device_id_type=MESH,
        )
        return target, remote, pltpu.make_async_copy(*here, local_sem.at[0])

    def wkv_copy(step, head, copy):
        slot = (step * local_heads + head) * repeats + copy
        other = lax.rem(me + step, sections)
        target = (other * local_heads + head) * repeats + copy
        here = (
            (wkv_ref if step == 0 else stage_wkv_ref.at[other]).at[:, pl.ds(head * width, width)],
            wkv_new_ref.at[pl.ds(pl.multiple_of(mine * block, 128), block), :],
        )
        remote = pltpu.make_async_remote_copy(
            *here,
            wkv_send.at[slot],
            wkv_recv.at[mine],
            device_id=(me, target),
            device_id_type=MESH,
        )
        return target, remote, pltpu.make_async_copy(*here, local_sem.at[1])

    every = [
        (make, step % sections, head, copy)
        for make in (page_copy, wkv_copy)
        for step in range(1, sections + 1)
        for head in range(local_heads)
        for copy in range(repeats)
    ]
    def begin(chosen):
        for make, step, head, copy in every:
            if step == chosen:
                target, remote, local = make(step, head, copy)
                pl.when(target != mine)(remote.start)
                pl.when(target == mine)(local.start)

    begin(0)

    for step in range(1, sections):
        other = lax.rem(me + step, sections)
        spread_copy(other, step).wait_send()
        pltpu.make_async_remote_copy(
            spread.at[other],
            spread.at[other],
            spread_send.at[step],
            spread_recv.at[other],
            device_id=(other, mine),
            device_id_type=MESH,
        ).wait_recv()

    tile = 256

    def product(i, carry):
        group = i // (columns // tile)
        span = pl.ds(pl.multiple_of(lax.rem(i, columns // tile) * tile, tile), tile)
        part[group, :, span] = jnp.dot(
            spread[group], wq_ref[:, span], preferred_element_type=jnp.float32
        )
        return carry

    lax.fori_loop(0, sections * (columns // tile), product, 0)
    for step in range(1, sections):
        part_copy(lax.rem(me + step, sections), step).start()
    partial_in[me] = part[me]

    for step in range(1, sections):
        other = lax.rem(me + step, sections)
        for which in range(2):
            stage_copy(me, other, step, which).wait_send()
            stage_copy(other, other, step, which).wait_recv()
        begin(step)

    for step in range(1, sections):

        def pass_on(i):
            for side in range(2):
                owner = me - step if side == 0 else me + step
                real = owner >= 0 if side == 0 else owner < sections

                @pl.when(real)
                def _():
                    relay_copy(owner, side, i).wait_recv()
                    pl.when(onward[side])(lambda: relay_copy(owner, side, i).start())

        each_chunk(pass_on)

    for step in range(1, sections):
        other = lax.rem(me + step, sections)
        part_copy(other, step).wait_send()
        pltpu.make_async_remote_copy(
            part.at[other],
            partial_in.at[other],
            part_send.at[step],
            part_recv.at[other],
            device_id=(other, mine),
            device_id_type=MESH,
        ).wait_recv()
    total = partial_in[0]
    for group in range(1, sections):
        total = total + partial_in[group]
    query_ref[...] = total

    keep.wait()

    def sent(i):
        for side in range(2):
            pl.when(onward[side])(lambda: own_copy(side, i).wait_send())
            for step in range(1, sections):
                owner = me - step if side == 0 else me + step
                real = owner >= 0 if side == 0 else owner < sections
                pl.when(jnp.logical_and(real, onward[side]))(
                    lambda: relay_copy(owner, side, i).wait_send()
                )

    each_chunk(sent)
    for make, step, head, copy in every:
        target, remote, local = make(step, head, copy)
        pl.when(target != mine)(remote.wait_send)
        pl.when(target == mine)(local.wait)
    for origin in range(tensors):
        pages_in = pltpu.make_async_remote_copy(
            pages_ref.at[0, 0],
            arrived_ref.at[origin],
            page_send.at[0],
            page_recv.at[origin],
            device_id=(me, origin),
            device_id_type=MESH,
        )
        wkv_in = pltpu.make_async_remote_copy(
            wkv_ref.at[:, pl.ds(0, width)],
            wkv_new_ref.at[pl.ds(origin * block, block), :],
            wkv_send.at[0],
            wkv_recv.at[origin],
            device_id=(me, origin),
            device_id_type=MESH,
        )
        outside = mine != origin
        pl.when(outside)(pages_in.wait_recv)
        pl.when(outside)(wkv_in.wait_recv)


def exchange(normed, wq_old, pages, wkv_old, sections, tensors, repeats):
    rows = normed.shape[0]
    depth, columns = wq_old.shape
    local_heads = pages.shape[1]
    width = pages.shape[4]
    copies = sections * local_heads * repeats
    dma = pltpu.SemaphoreType.DMA
    vmem = pl.BlockSpec(memory_space=pltpu.VMEM)
    hbm = pl.BlockSpec(memory_space=pl.ANY)
    return pl.pallas_call(
        functools.partial(exchange_kernel, sections, tensors, local_heads, repeats),
        out_shape=(
            jax.ShapeDtypeStruct((rows, columns), jnp.float32),
            jax.ShapeDtypeStruct((tensors,) + pages.shape[2:], pages.dtype),
            jax.ShapeDtypeStruct((wkv_old.shape[0] * tensors, width), wkv_old.dtype),
            jax.ShapeDtypeStruct((depth * sections, columns), wq_old.dtype),
            jax.ShapeDtypeStruct(pages.shape, pages.dtype),
            jax.ShapeDtypeStruct((sections,) + wkv_old.shape, wkv_old.dtype),
        ),
        in_specs=[vmem, vmem, hbm, hbm],
        out_specs=(vmem, hbm, hbm, hbm, hbm, hbm),
        scratch_shapes=[
            pltpu.VMEM((sections, rows, depth), normed.dtype),
            pltpu.VMEM((sections, rows, columns), jnp.float32),
            pltpu.VMEM((sections, rows, columns), jnp.float32),
            dma((sections,)),
            dma((sections,)),
            dma((sections,)),
            dma((sections,)),
            dma((copies,)),
            dma((tensors,)),
            dma((copies,)),
            dma((tensors,)),
            dma((3,)),
            dma((2, CHUNKS)),
            dma((sections, CHUNKS)),
            dma((sections, CHUNKS)),
            dma((2, sections)),
            dma((2, sections)),
        ],
        compiler_params=pltpu.CompilerParams(
            has_side_effects=True, vmem_limit_bytes=40 * 2**20
        ),
        cost_estimate=pl.CostEstimate(
            flops=2 * sections * rows * depth * columns,
            bytes_accessed=400 * 2**20,
            transcendentals=0,
        ),
        name="exchange",
    )(normed, wq_old, pages, wkv_old)


def attend_kernel(
    pages_of, per_block, page, head_dim, place_ref, length_ref, in_ref, fresh_ref, query_ref, cache_ref, context_ref
):
    request = pl.program_id(0)
    length = length_ref[request]
    base = request * pages_of

    def order(j, carry):
        spot = place_ref[base + j]
        start = pl.multiple_of(j * page, page)
        cache_ref[0, pl.ds(start, page), :] = in_ref[
            lax.div(spot, per_block), 0, lax.rem(spot, per_block)
        ]
        return carry

    lax.fori_loop(0, pages_of, order, 0, unroll=8)
    start = pl.multiple_of(lax.div(length, page) * page, page)
    held = cache_ref[0, pl.ds(start, page), :]
    row = lax.broadcasted_iota(jnp.int32, held.shape, 0)
    fresh = jnp.broadcast_to(fresh_ref[0].astype(jnp.float32), held.shape)
    cache_ref[0, pl.ds(start, page), :] = jnp.where(
        row == lax.rem(length, page), fresh, held.astype(jnp.float32)
    ).astype(held.dtype)
    keys = cache_ref[0, :, :head_dim]
    values = cache_ref[0, :, head_dim:]
    scores = lax.dot_general(
        query_ref[0], keys, (((1,), (1,)), ((), ())), preferred_element_type=jnp.float32
    ) * head_dim ** (-0.5)
    seen = lax.broadcasted_iota(jnp.int32, scores.shape, 1) <= length
    peak = jnp.max(jnp.where(seen, scores, -jnp.inf), axis=1, keepdims=True)
    weights = jnp.where(seen, jnp.exp(scores - peak), 0.0)
    probs = (weights / jnp.sum(weights, axis=1, keepdims=True)).astype(jnp.bfloat16)
    context_ref[0] = jnp.dot(probs, values, preferred_element_type=jnp.float32).astype(
        context_ref.dtype
    )


def attend(arrived, place, lengths, fresh, query, head_dim):
    blocks, rows, per_block, page, width = arrived.shape
    pages_of = blocks * per_block
    heads = query.shape[1]
    return pl.pallas_call(
        functools.partial(attend_kernel, pages_of, per_block, page, head_dim),
        out_shape=(
            jax.ShapeDtypeStruct((rows, pages_of * page, width), arrived.dtype),
            jax.ShapeDtypeStruct(query.shape, jnp.bfloat16),
        ),
        grid_spec=pltpu.PrefetchScalarGridSpec(
            num_scalar_prefetch=2,
            grid=(rows,),
            in_specs=[
                pl.BlockSpec((blocks, 1, per_block, page, width), lambda r, *_: (0, r, 0, 0, 0)),
                pl.BlockSpec((1, 1, width), lambda r, *_: (r, 0, 0)),
                pl.BlockSpec((1, heads, head_dim), lambda r, *_: (r, 0, 0)),
            ],
            out_specs=(
                pl.BlockSpec((1, pages_of * page, width), lambda r, *_: (r, 0, 0)),
                pl.BlockSpec((1, heads, head_dim), lambda r, *_: (r, 0, 0)),
            ),
        ),
        cost_estimate=pl.CostEstimate(
            flops=4 * rows * heads * pages_of * page * head_dim,
            bytes_accessed=4 * arrived.size,
            transcendentals=rows * heads * pages_of * page,
        ),
        compiler_params=pltpu.CompilerParams(vmem_limit_bytes=40 * 2**20),
        name="attend",
    )(place.reshape(-1), lengths, arrived, fresh[:, None, :], query)


def shards(hidden_state, norm_gain, wq_old, wkv_old, kv_old, page_table, lengths):
    sections = lax.axis_size("section")
    tensors = lax.axis_size("tensor")
    section_id = lax.axis_index("section")
    tensor_id = lax.axis_index("tensor")
    rows = hidden_state.shape[0]
    head_dim = HEAD_DIM
    width = 2 * head_dim
    repeats = tensors // KV_HEADS
    queries_here = wq_old.shape[1] // head_dim
    pool_dev = kv_old.shape[1]
    page = kv_old.shape[2]
    per_block = page_table.shape[1] // tensors
    widened = hidden_state.astype(jnp.float32)
    scale = lax.rsqrt(jnp.mean(widened * widened, axis=1, keepdims=True) + EPSILON)
    normed = (widened * scale * norm_gain[None, :]).astype(jnp.bfloat16)
    owner = page_table // pool_dev
    blocks = jnp.arange(tensors, dtype=jnp.int32)
    onehot = (owner[:, :, None] == blocks[None, None, :]).astype(jnp.int32)
    ranks = jnp.sum((jnp.cumsum(onehot, axis=1) - 1) * onehot, axis=2)
    mine = owner == tensor_id
    wanted = ranks[:, :, None] == jnp.arange(per_block, dtype=jnp.int32)[None, None, :]
    picks = (mine[:, :, None] & wanted).astype(jnp.int32)
    spots = jnp.sum(picks * (page_table % pool_dev)[:, :, None], axis=1)
    pages = pick_pages(kv_old, spots.reshape(-1), sections)
    query, arrived, wkv_new, wq_new, _, _ = exchange(
        normed, wq_old, pages, wkv_old, sections, tensors, repeats
    )
    arrived = arrived.reshape(tensors, rows, per_block, page, width)
    place = lax.dynamic_slice_in_dim(owner * per_block + ranks, section_id * rows, rows, 0)
    my_lengths = lax.dynamic_slice_in_dim(lengths, section_id * rows, rows, 0)
    fresh = jnp.dot(normed, wkv_new, preferred_element_type=jnp.float32)
    fresh_key = rotate(fresh[:, None, :head_dim], my_lengths, head_dim)[:, 0]
    fresh = jnp.concatenate([fresh_key, fresh[:, head_dim:]], axis=1).astype(jnp.bfloat16)
    query = rotate(query.reshape(rows, queries_here, head_dim), my_lengths, head_dim).astype(
        jnp.bfloat16
    )
    cache, context = attend(arrived, place, my_lengths, fresh, query, head_dim)
    return (context.reshape(rows, queries_here * head_dim), cache[:, None], wq_new, wkv_new)


def solution(mesh):
    placed = (
        P("section", None),
        P(),
        P("section", "tensor"),
        P("tensor", "section"),
        P("section", "tensor", None, None),
        P(),
        P(),
    )
    return jax.shard_map(
        shards,
        mesh=mesh,
        in_specs=placed,
        out_specs=(
            P("section", "tensor"),
            P("section", "tensor", None, None),
            P(None, "tensor"),
            P(None, "tensor"),
        ),
        check_vma=False,
    )
```

time: 691 us -> 549 us (0.79)
  Pallas kernels: 0 us -> 515 us
  blocking collectives: 370 us -> 0 us
  waiting for transfers between devices: 158 us -> 0 us
  local copies, waits for them, and re-layouts: 88.8 us -> 24.5 us
  other arithmetic: 37.3 us -> 8.23 us
  between operations: 15.8 us -> 0.78 us
  starting transfers between devices: 11.7 us -> 0 us
  matrix products: 8.55 us -> 0.65 us
    pallas_call x0 -> x3, Pallas kernels: none -> 515 us  [the longest x1 492 us: exchange(): pl.pallas_call(functools.partial(exchange_kernel, sections, tensors, loca...]
    all_to_all x1 -> x0, blocking collectives: 370 us -> none  [shards(): lax.all_to_all(copied, 'section', split_axis=1, concat_axis=0, tiled=True)]
    all_to_all x2 -> x0, waiting for transfers between devices: 97.4 us -> none  [the longest x1 88.5 us: shards(): lax.all_to_all(lax.all_to_all(copied, 'section', split_axis=1, concat_axi...]
    all_gather x2 -> x0, waiting for transfers between devices: 59.3 us -> none  [the longest x1 36.9 us: shards(): kv_rows = lax.all_gather(wkv_old, 'tensor', axis=0, tiled=True)]
    gather x5 -> x0, local copies, waits for them, and re-layouts: 45.6 us -> none  [the longest x2 30.9 us: shards(): pages = jnp.take(kv_old, spots.reshape(-1), axis=1)]
    select_n x5 -> x0, other arithmetic: 26.8 us -> none  [the longest x2 14.4 us: shards(): cache = jnp.where(written, fresh[:, None, :], ordered)]
    all_to_all x3 -> x0, local copies, waits for them, and re-layouts: 16.5 us -> none  [the longest x1 7.89 us: shards(): lax.all_to_all(lax.all_to_all(copied, 'section', split_axis=1, concat_axi...]
    all_to_all x2 -> x0, starting transfers between devices: 11.6 us -> none  [the longest x1 6.35 us: shards(): lax.all_to_all(normed, 'section', split_axis=1, concat_axis=0, tiled=True)]
  transfers between devices with their start and end apart: 6 -> 0, of which waited for: 4 -> 0; matrix products, arithmetic and copies ran while one was open for 17% -> 0% of each run, Pallas kernels for 0% -> 0%
where the time goes in v1:
time: 549 us
  Pallas kernels  515 us (94%)
  local copies, waits for them, and re-layouts  24.5 us (4%)
  other arithmetic  8.23 us (1%)
    pallas_call x1, Pallas kernels, exchange(): pl.pallas_call(functools.partial(exchange_kernel, sections, tensors, loca...  492 us
    unnamed x13, local copies, waits for them, and re-layouts  24.2 us
    pallas_call x1, Pallas kernels, attend(): pl.pallas_call(functools.partial(attend_kernel, pages_of, per_block, page...  15.9 us

profile of v1, /device:TPU:0, one launch (start us, length us, event | category | flops | bytes accessed | tf_op | source)
XLA Modules:
  0.0 549.1 jit_solution(5833586532725514584)
XLA Ops:
  0.6 0.8 copy.35
  1.5 2.3 select_reduce_fusion.1
  3.8 0.1 dynamic-slice_add_fusion
  3.9 0.1 copy.39
  3.9 0.1 reshape.170.place_ref
  4.0 0.7 fusion.10
  4.7 1.1 fusion.4
  5.9 1.1 fusion.6.normed_ref
  7.0 2.2 select_reduce_fusion
  9.2 0.1 reshape.171.spots_ref
  9.3 0.0 copy-start.2
  9.3 0.0 copy-start.3
  9.3 7.0 %pick_pages.1.pages_ref = bf16[4,2,128,16,256]{4,3,2,1,0:T(8,128)(2,1)S(1)} custom-call(s32[512]{0:T(512)S(1)} %reshape.171.spots_ref, bf16[2,512,16,256]{3,2,1,0:T(8,128)(2,1)} %kv_ref.1), custom_call_target="tpu_custom_call" | custom-call | tf_op jit(solution)/shard_map/pick_pages/pallas_call | solution.py:46
  16.3 0.0 copy-start
  16.3 3.4 copy-done
  19.7 0.0 copy-done.2
  19.7 0.0 copy-done.3
  19.7 492.0 %exchange.1 = (f32[16,1024]{1,0:T(8,128)S(1)}, bf16[8,128,16,256]{3,2,1,0:T(8,128)(2,1)}, bf16[8192,256]{1,0:T(8,128)(2,1)S(1)}, bf16[8192,1024]{1,0:T(8,128)(2,...) custom-call(bf16[16,8192]{1,0:T(8,128)(2,1)S(1)} %fusion.6.normed_ref, ...), custom_call_target="tpu_custom_call" | custom-call | flops 268435456 | bytes 419430400 | tf_op jit(solution)/shard_map/exchange/pallas_call | solution.py:346
  511.8 0.7 fusion.11
  512.5 0.1 mul.133
  512.5 0.3 subtract_convert_fusion.1
  512.8 0.1 pad_maximum_fusion.1.fresh_ref
  512.9 0.1 multiply_cosine_fusion
  513.1 0.1 subtract_convert_fusion
  513.2 0.1 pad_maximum_fusion.query_ref
  513.3 0.0 copy-start.1
  513.3 3.4 copy-done.1
  516.6 15.9 %attend.1 = (bf16[16,1024,256]{2,1,0:T(8,128)(2,1)}, bf16[16,8,128]{2,1,0:T(8,128)(2,1)S(1)}) custom-call(s32[1024]{0:T(1024)S(1)} %reshape.170.place_ref, s32[16]{0:T(128)S(1)} %get-tuple-element.37.length_ref, bf16[8,16,8,16,256]{4,3,2,1,0:T(8,128)(2,1)S(1)} %bitcast.16, bf16[16,1,256]{2,1,0:T(2,128)(2,1)S(1)} %pad_maximum_fusion.1.fresh_ref, ...), custom_call_target="tpu_custom_call" | custom-call | flops 67108864 | bytes 16777216 | tf_op jit(solution)/shard_map/attend/pallas_call | solution.py:430
  532.5 0.6 copy.46
  533.2 13.9 %copy.49 = bf16[8192,1024]{1,0:T(8,128)(2,1)} copy(bf16[8192,1024]{1,0:T(8,128)(2,1)} %get-tuple-element.52) | data formatting | bytes 33554432
  547.1 2.0 copy.50
  (8 shorter events, 0.1 us)
Async XLA Ops:
  9.3 10.4 %copy-start.2 = (bf16[2048,1024]{1,0:T(8,128)(2,1)S(1)}, bf16[2048,1024]{1,0:T(8,128)(2,1)}, u32[]{:S(2)}) copy-start(bf16[2048,1024]{1,0:T(8,128)(2,1)} %wq_ref.1) | copy-start | bytes 12582916
  9.3 10.4 %copy-start.3 = (bf16[1024,512]{1,0:T(8,128)(2,1)S(1)}, bf16[1024,512]{1,0:T(8,128)(2,1)}, u32[]{:S(2)}) copy-start(bf16[1024,512]{1,0:T(8,128)(2,1)} %wkv_ref.1) | copy-start | bytes 3145732
  16.3 3.4 copy-start
  513.3 3.4 copy-start.1
